TPU v7x, 256 devices: a whole 4x4x8 slice. The times are simulated.
256 devices in a mesh: ra: 16 (over x_hi, y, core), dec: 16 (over z, x_lo).
Axes of the slice: x: 4 (x_hi: 2, x_lo: 2; x = x_hi * 2 + x_lo), y: 4, z: 8, core: 2. Of those that a mesh axis runs over, the one named last changes fastest.
Arguments:
- design: float32 [5, 80, 64, 4096], P(None, None, 'ra', 'dec'), may hold values from -6 to 6
- observed: float32 [80, 64, 4096], P(None, 'ra', 'dec'), may hold values from -6 to 6
- weight: float32 [80, 64, 4096], P(None, 'ra', 'dec'), may hold values from 0.3 to 3
- params: float32 [5, 64, 4096], P(None, 'ra', 'dec'), may hold values from -4 to 4
- offsets: int32 [80, 64, 4096], P(None, 'ra', 'dec'), may hold values from 0 to 8, as said below
- counts: int32 [64, 4096], P('ra', 'dec'), may hold values from 10 to 80, as said below
Outputs:
- new_params: float32 [5, 64, 4096], P(None, 'ra', 'dec')
- reduced_chi: float32 [], replicated
Inputs may be any that keep to these rules, and one draw needn't show every extreme that they name: `offsets`: in the first and the last latitude row of cells no offset steps outside the grid in latitude. `counts`: cells near the middle latitude hold more live observations; the two middle latitude rows hold 80.
All inputs are finite; a program needn't handle non-finite values.
Results may differ from a plain program's by a relative error of at most 0.0003.
Values sent between devices are 32-bit elements; how exact they have to be, the bound alone decides.
No kernel may reach another device: no remote copies, remote signals or barrier semaphores. Data moves between devices by JAX's collectives and lax.ppermute only.
A program may use at most 64 MiB of HBM per device.

v0:
```python
import jax
import jax.numpy as jnp
from jax import lax
from jax.sharding import Mesh
from jax.sharding import PartitionSpec as P

RA_DEC = ("ra_0", "ra_1", "ra_2", "dec_0", "dec_1")
RA = ("ra_0", "ra_1", "ra_2")
DEC = ("dec_0", "dec_1")


def extended_2(cells, sides, width):
    for axis, dim in sides:
        count = lax.axis_size(axis)
        head = lax.slice_in_dim(cells, 0, width, axis=dim)
        tail = lax.slice_in_dim(cells, cells.shape[dim] - width, cells.shape[dim], axis=dim)
        cells = jnp.concatenate(
            [
                lax.ppermute(tail, axis, [(i, (i + 1) % count) for i in range(count)]),
                cells,
                lax.ppermute(head, axis, [((i + 1) % count, i) for i in range(count)]),
            ],
            axis=dim,
        )
    return cells


def over_axes(value, axes):
    for axis in axes:
        value = lax.psum(value, axis)
    return value


def pair_list():
    pairs = []
    for first in range(5):
        for second in range(first, 5):
            pairs.append((first, second))
    return pairs


def code_sums(design, observed, masked_weight, codes, windows):
    source = windows[0][:, None]
    for code in range(1, 9):
        source = jnp.where((codes == code)[None], windows[code][:, None], source)
    resid = observed
    for comp in range(5):
        resid = resid - design[comp] * source[comp]
    weighted = masked_weight * resid
    products = []
    for comp in range(5):
        products.append(design[comp] * weighted)
    for first, second in pair_list():
        products.append(masked_weight * design[first] * design[second])
    binned = []
    for code in range(9):
        hit = codes == code
        binned.append(
            jnp.stack([jnp.sum(jnp.where(hit, prod, 0.0), axis=0) for prod in products], axis=0)
        )
    return (binned, jnp.sum(weighted * resid))


def solve_blocks(stacked):
    rhs = [stacked[comp] for comp in range(5)]
    normal = [[None] * 5 for item in range(5)]
    for place, pair in enumerate(pair_list()):
        first, second = pair
        value = stacked[5 + place]
        if first == second:
            value = value + 1.0
        normal[first][second] = value
        normal[second][first] = value
    lower = [[None] * 5 for item in range(5)]
    for first in range(5):
        for second in range(first + 1):
            running = normal[first][second]
            for inner in range(second):
                running = running - lower[first][inner] * lower[second][inner]
            if first == second:
                lower[first][first] = jnp.sqrt(running)
            else:
                lower[first][second] = running / lower[second][second]
    forward = []
    for first in range(5):
        running = rhs[first]
        for inner in range(first):
            running = running - lower[first][inner] * forward[inner]
        forward.append(running / lower[first][first])
    answer = [None] * 5
    for first in range(4, -1, -1):
        running = forward[first]
        for inner in range(first + 1, 5):
            running = running - lower[inner][first] * answer[inner]
        answer[first] = running / lower[first][first]
    return jnp.stack(answer, axis=0)


def per_device(design, observed, weight, params, offsets, counts):
    cells_ra = params.shape[1]
    cells_dec = params.shape[2]
    slots = lax.broadcasted_iota(jnp.int32, observed.shape, 0)
    codes = jnp.where(slots < counts[None], offsets, 9)
    floats = jnp.concatenate([design, observed[None], weight[None]], axis=0)
    extended, extended_codes = (
        extended_2(floats, ((RA, 2), (DEC, 3)), 1),
        extended_2(codes[None], ((RA, 2), (DEC, 3)), 1),
    )
    ext_codes = extended_codes[0]
    padded_local = jnp.pad(params, ((0, 0), (2, 2), (2, 2)))
    windows = []
    for code in range(9):
        step_ra = code // 3 - 1
        step_dec = code % 3 - 1
        windows.append(
            padded_local[
                :, 1 + step_ra : 3 + step_ra + cells_ra, 1 + step_dec : 3 + step_dec + cells_dec
            ]
        )
    step_ra_all = ext_codes // 3 - 1
    step_dec_all = ext_codes % 3 - 1
    place_ra = lax.broadcasted_iota(jnp.int32, ext_codes.shape, 1) - 1 + step_ra_all
    place_dec = lax.broadcasted_iota(jnp.int32, ext_codes.shape, 2) - 1 + step_dec_all
    owned = (
        (place_ra >= 0)
        & (place_ra < cells_ra)
        & (place_dec >= 0)
        & (place_dec < cells_dec)
        & (ext_codes < 9)
    )
    masked_weight = jnp.where(owned, extended[6], jnp.zeros_like(extended[6]))
    binned, chi = code_sums(extended[:5], extended[5], masked_weight, ext_codes, windows)
    total = jnp.zeros((20, cells_ra, cells_dec), jnp.float32)
    for code in range(9):
        step_ra = code // 3 - 1
        step_dec = code % 3 - 1
        total = (
            total
            + binned[code][
                :, 1 - step_ra : 1 - step_ra + cells_ra, 1 - step_dec : 1 - step_dec + cells_dec
            ]
        )
    live_count = jnp.sum(counts).astype(jnp.float32)
    chi_total, count_total = (over_axes(chi, RA_DEC), over_axes(live_count, RA_DEC))
    new_params = params + solve_blocks(total)
    return (new_params, chi_total / count_total)


def solution(mesh):
    finer = Mesh(mesh.devices.reshape(2, 4, 2, 8, 2), ("ra_0", "ra_1", "ra_2", "dec_0", "dec_1"))
    return jax.shard_map(
        per_device,
        mesh=finer,
        in_specs=(
            P(None, None, RA, DEC),
            P(None, RA, DEC),
            P(None, RA, DEC),
            P(None, RA, DEC),
            P(None, RA, DEC),
            P(RA, DEC),
        ),
        out_specs=(P(None, RA, DEC), P()),
        check_vma=False,
    )
```

profile of v0, /device:TPU:14, one launch (start us, length us, event | category | flops | bytes accessed | tf_op | source)
XLA Modules:
  0.0 148.5 jit_solution(16316700984926354208)
XLA Ops:
  0.7 1.1 fusion.38
  1.9 1.7 %collective-permute-start.1 = (s32[1,80,1,256]{3,1,2,0:T(8,128)S(1)}, s32[1,80,1,256]{3,1,2,0:T(8,128)S(1)}, u32[]{:S(2)}, u32[]{:S(2)}) collective-permute-start(s32[1,80,1,256]{3,1,2,0:T(8,128)S(1)} %get-tuple-element.1082), channel_id=1, source_target_pairs={{16,0},{32,16},{48,32},{64,48},{80,64},{96,80},{112,96},{128,112},... | collective-permute-start | bytes 245768 | tf_op jit(solution)/shard_map/ppermute | solution.py:21
  3.6 1.7 %copy.21 = f32[5,80,4,256]{3,1,2,0:T(8,128)S(1)} copy(f32[5,80,4,256]{3,2,1,0:T(4,128)} %param.6) | data formatting | bytes 3276800 | tf_op args[0]
  5.5 1.2 pad_maximum_fusion.4
  6.8 1.7 %collective-permute-start.5 = (f32[7,80,1,256]{3,1,2,0:T(8,128)}, f32[7,80,1,256]{3,1,2,0:T(8,128)S(1)}, u32[]{:S(2)}, u32[]{:S(2)}) collective-permute-start(f32[7,80,1,256]{3,1,2,0:T(8,128)} %get-tuple-element.1069), channel_id=1, source_target_pairs={{16,0},{32,16},{48,32},{64,48},{80,64},{96,80},{112,96},{128,112},... | collective-permute-start | bytes 1720328 | tf_op jit(solution)/shard_map/ppermute | solution.py:21
  8.5 0.9 pad_slice_fusion.8
  9.5 0.9 fusion.75
  10.3 0.8 fusion.85
  11.2 2.2 %collective-permute-start.2 = (s32[1,80,6,1]{3,1,2,0:T(8,128)}, s32[1,80,6,1]{3,1,2,0:T(8,128)}, u32[]{:S(2)}, u32[]{:S(2)}) collective-permute-start(s32[1,80,6,1]{3,1,2,0:T(8,128)} %get-tuple-element.1077), channel_id=1, source_target_pairs={{0,1},{1,2},{2,3},{3,4},{4,5},{5,6},{6,7},{7,8},{8,9},{9,10},{10,1... | collective-permute-start | bytes 5768 | tf_op jit(solution)/shard_map/ppermute | solution.py:19
  14.7 9.9 %collective-permute-done.2 = s32[1,80,6,1]{3,1,2,0:T(8,128)} collective-permute-done((s32[1,80,6,1]{3,1,2,0:T(8,128)}, s32[1,80,6,1]{3,1,2,0:T(8,128)}, u32[]{:S(2)}, u32[]{:S(2)}) %collective-permute-start.2) | collective-permute-done | bytes 1952 | tf_op jit(solution)/shard_map/ppermute | solution.py:19
  24.6 2.2 %broadcast_compare_fusion.11 = (pred[80,6,258]{2,0,1:T(8,128)(4,1)}, s32[80,6,258]{2,0,1:T(8,128)S(1)}) fusion(s32[80,6,1]{2,0,1:T(8,128)} %bitcast.13, s32[80,6,256]{2,0,1:T(8,128)} %get-tuple-element.1079, s32[80,6,1]{2,0,1:T(8,128)} %bitcast.11), kind=kLoop, calls=%fused_computation.445 | loop fusion | flops 371520 | bytes 1114560 | tf_op jit(solution)/shard_map/eq | solution.py:45
  26.8 1.6 %broadcast_compare_fusion.10 = (pred[80,6,258]{2,0,1:T(8,128)(4,1)}, pred[80,6,258]{2,0,1:T(8,128)(4,1)}, pred[80,6,258]{2,0,1:T(8,128)(4,1)}, pred[80,6,258]{2,...) fusion(s32[80,6,258]{2,0,1:T(8,128)S(1)} %get-tuple-element.1037), kind=kLoop, calls=%fused_computation.444 | loop fusion | flops 866880 | bytes 1362240 | tf_op jit(solution)/shard_map/eq | solution.py:45
  28.4 0.8 copy-done.5
  29.3 0.8 copy-done.6
  30.3 1.8 %fusion.84 = (f32[7,80,6,1]{3,1,2,0:T(8,128)}, f32[7,80,6,1]{3,1,2,0:T(8,128)S(1)}) fusion(f32[7,80,6,256]{3,1,2,0:T(8,128)S(1)} %pad_maximum_fusion.1), kind=kLoop, calls=%fused_computation.535 | loop fusion | bytes 53760 | tf_op jit(solution)/shard_map/slice | solution.py:16
  32.1 2.6 %copy.22 = f32[7,80,6,1]{1,3,2,0:T(1,128)} copy(f32[7,80,6,1]{3,1,2,0:T(8,128)} %get-tuple-element.1066) | data formatting | bytes 26880 | tf_op jit(solution)/shard_map/slice | solution.py:16
  34.7 1.1 copy.23
  35.8 2.2 %collective-permute-start.7 = (f32[7,80,6,1]{1,3,2,0:T(1,128)}, f32[7,80,6,1]{1,3,2,0:T(1,128)}, u32[]{:S(2)}, u32[]{:S(2)}) collective-permute-start(f32[7,80,6,1]{1,3,2,0:T(1,128)} %copy.23), channel_id=1, source_target_pairs={{1,0},{2,1},{3,2},{4,3},{5,4},{6,5},{7,6},{8,7},{9,8},{10,9},{11,1... | collective-permute-start | bytes 40328 | tf_op jit(solution)/shard_map/ppermute | solution.py:21
  38.0 0.9 collective-permute-start.6
  38.9 5.6 %select_select_fusion = f32[5,80,6,258]{3,1,2,0:T(8,128)} fusion(f32[5,6,258]{2,1,0:T(8,128)} %get-tuple-element.1094, f32[5,6,258]{2,1,0:T(8,128)} %get-tuple-element.1093, f32[5,6,258]{2,1,0:T(8,128)} %get-tuple-element.1092, f32[5,6,258]{2,1,0:T(8,128)} %get-tuple-element.1091, f32[5,6,258]{2,1,0:T(8,128)} %get-tuple-element.1090, ...), kind=kLoop, calls=%fused_computation.1 | loop fusion | flops 4953600 | bytes 3746160 | tf_op jit(solution)/shard_map/jit(_where)/select_n | solution.py:45
  45.2 1.3 copy.24
  46.5 2.5 %copy.25 = f32[7,80,6,1]{3,1,2,0:T(8,128)} copy(f32[7,80,6,1]{1,3,2,0:T(1,128)} %collective-permute-done.7) | data formatting | bytes 26880 | tf_op jit(solution)/shard_map/ppermute | solution.py:21
  49.0 5.6 %pad_maximum_fusion = f32[7,80,6,258]{3,1,2,0:T(8,128)S(1)} fusion(f32[7,80,6,1]{3,1,2,0:T(8,128)} %copy.25, f32[7,80,1,256]{3,1,2,0:T(8,128)} %copy-done.6, f32[1,80,4,256]{3,1,2,0:T(8,128)} %copy-done.1, f32[1,80,4,256]{3,1,2,0:T(8,128)} %copy-done.2, f32[5,80,4,256]{3,1,2,0:T(8,128)S(1)} %copy.21, f32[7,80,1,256]{3,1,2,0:T(8,128)} %copy-done.5, ...), kind=kLoop, calls=%fused_computation | loop fusion | flops 5201280 | bytes 6935040 | tf_op jit(solution)/shard_map/concatenate | solution.py:17
  54.6 3.3 %multiply_reduce_fusion = (f32[]{:T(128)}, f32[80,6,258]{2,0,1:T(8,128)S(1)}, f32[80,6,258]{2,0,1:T(8,128)S(1)}, s32[1,80,6,258]{3,1,2,0:T(8,128)S(1)}) fusion(f32[7,80,6,258]{3,1,2,0:T(8,128)S(1)} %pad_maximum_fusion, s32[258]{0:T(512)S(1)} %iota_add_fusion, s32[6]{0:T(128)S(1)} %iota_add_fusion.1, s32[1,80,6,1]{3,1,2,0:T(8,128)} %collective-permute-done.3, ...), kind=kLoop, calls=%fused_computation.37 | loop fusion | flops 5325119 | bytes 7926820 | tf_op jit(solution)/shard_map/reduce_sum | solution.py:61
  58.6 0.8 fusion.32
  59.4 15.2 %select_reduce_fusion.169 = (f32[6,258]{1,0:T(8,128)S(1)}, f32[6,258]{1,0:T(8,128)S(1)}, f32[6,258]{1,0:T(8,128)S(1)}, f32[6,258]{1,0:T(8,128)S(1)}, f32[6,258]{...) fusion(f32[80,6,258]{2,0,1:T(8,128)S(1)} %get-tuple-element.105, ...), kind=kLoop, calls=%fused_computation.207 | loop fusion | flops 23266440 | bytes 7120800 | tf_op jit(solution)/shard_map/reduce_sum | solution.py:59
  74.6 14.1 %select_reduce_fusion.179 = (f32[6,258]{1,0:T(8,128)S(1)}, f32[6,258]{1,0:T(8,128)S(1)}, f32[6,258]{1,0:T(8,128)S(1)}, f32[6,258]{1,0:T(8,128)S(1)}, f32[6,258]{...) fusion(f32[80,6,258]{2,0,1:T(8,128)S(1)} %get-tuple-element.106, ...), kind=kLoop, calls=%fused_computation.217 | loop fusion | flops 22151880 | bytes 6625440 | tf_op jit(solution)/shard_map/reduce_sum | solution.py:59
  91.9 7.1 %all-reduce.5 = (f32[]{:T(128)}, f32[]{:T(128)}) all-reduce(f32[]{:T(128)} %get-tuple-element.1002, f32[]{:T(128)S(6)} %convert_element_type.5), channel_id=1, replica_groups=mesh['ra_0'=2,'ra_1'=4,'ra_2'=2,'dec_0'=8,'dec_1'=2] {'ra_0'}, use_global_device_ids=true, to_apply=%region_181.182 | all-reduce | flops 2 | bytes 16 | tf_op jit(solution)/shard_map/psum | solution.py:30
  99.0 17.4 %all-reduce.2 = (f32[]{:T(128)}, f32[]{:T(128)}) all-reduce(f32[]{:T(128)} %get-tuple-element.1000, f32[]{:T(128)} %get-tuple-element.1001), channel_id=1, replica_groups=mesh['ra_0'=2,'ra_1'=4,'ra_2'=2,'dec_0'=8,'dec_1'=2] {'ra_1'}, use_global_device_ids=true, to_apply=%region_182.183 | all-reduce | flops 2 | bytes 16 | tf_op jit(solution)/shard_map/psum | solution.py:30
  116.4 3.1 %all-reduce.4 = (f32[]{:T(128)}, f32[]{:T(128)}) all-reduce(f32[]{:T(128)} %get-tuple-element.994, f32[]{:T(128)} %get-tuple-element.995), channel_id=1, replica_groups=mesh['ra_0'=2,'ra_1'=4,'ra_2'=2,'dec_0'=8,'dec_1'=2] {'ra_2'}, use_global_device_ids=true, to_apply=%region_183.184 | all-reduce | flops 2 | bytes 16 | tf_op jit(solution)/shard_map/psum | solution.py:30
  119.5 21.1 %all-reduce.1 = (f32[]{:T(128)}, f32[]{:T(128)}) all-reduce(f32[]{:T(128)} %get-tuple-element.998, f32[]{:T(128)} %get-tuple-element.999), channel_id=1, replica_groups=mesh['ra_0'=2,'ra_1'=4,'ra_2'=2,'dec_0'=8,'dec_1'=2] {'dec_0'}, use_global_device_ids=true, to_apply=%region_184.185 | all-reduce | flops 2 | bytes 16 | tf_op jit(solution)/shard_map/psum | solution.py:30
  140.6 5.5 %all-reduce.3 = (f32[]{:T(128)}, f32[]{:T(128)}) all-reduce(f32[]{:T(128)} %get-tuple-element.992, f32[]{:T(128)} %get-tuple-element.993), channel_id=1, replica_groups=mesh['ra_0'=2,'ra_1'=4,'ra_2'=2,'dec_0'=8,'dec_1'=2] {'dec_1'}, use_global_device_ids=true, to_apply=%region_185.186 | all-reduce | flops 2 | bytes 16 | tf_op jit(solution)/shard_map/psum | solution.py:30
  (238 shorter events, 4.2 us)
Async XLA Ops:
  0.6 4.7 %copy-start.12 = (f32[80,4,256]{2,1,0:T(4,128)S(1)}, f32[80,4,256]{2,1,0:T(4,128)}, u32[]{:S(2)}) copy-start(f32[80,4,256]{2,1,0:T(4,128)} %param.8) | copy-start | bytes 983044
  0.6 4.7 %copy-start.13 = (f32[80,4,256]{2,1,0:T(4,128)S(1)}, f32[80,4,256]{2,1,0:T(4,128)}, u32[]{:S(2)}) copy-start(f32[80,4,256]{2,1,0:T(4,128)} %param.7) | copy-start | bytes 983044
  1.8 7.7 %copy-start.3 = (s32[1,80,4,256]{3,1,2,0:T(8,128)}, s32[1,80,4,256]{3,1,2,0:T(8,128)S(1)}, u32[]{:S(2)}) copy-start(s32[1,80,4,256]{3,1,2,0:T(8,128)S(1)} %fusion.38) | copy-start | bytes 983044
  1.8 7.6 %collective-permute-start = (s32[1,80,1,256]{3,1,2,0:T(8,128)S(1)}, s32[1,80,1,256]{3,1,2,0:T(8,128)S(1)}, u32[]{:S(2)}, u32[]{:S(2)}) collective-permute-start(s32[1,80,1,256]{3,1,2,0:T(8,128)S(1)} %get-tuple-element.1081), channel_id=1, source_target_pairs={{0,16},{16,32},{32,48},{48,64},{64,80},{80,96},{96,112},{112,128},... | collective-permute-start | bytes 245768 | tf_op jit(solution)/shard_map/ppermute | solution.py:19
  1.9 6.6 %copy-start.14 = (f32[5,4,256]{2,1,0:T(4,128)S(1)}, f32[5,4,256]{2,1,0:T(4,128)}, u32[]{:S(2)}) copy-start(f32[5,4,256]{2,1,0:T(4,128)} %param.9) | copy-start | bytes 61444
  1.9 7.6 %collective-permute-start.1 = (s32[1,80,1,256]{3,1,2,0:T(8,128)S(1)}, s32[1,80,1,256]{3,1,2,0:T(8,128)S(1)}, u32[]{:S(2)}, u32[]{:S(2)}) collective-permute-start(s32[1,80,1,256]{3,1,2,0:T(8,128)S(1)} %get-tuple-element.1082), channel_id=1, source_target_pairs={{16,0},{32,16},{48,32},{64,48},{80,64},{96,80},{112,96},{128,112},... | collective-permute-start | bytes 245768 | tf_op jit(solution)/shard_map/ppermute | solution.py:21
  5.4 8.0 %copy-start.16 = (s32[4,256]{1,0:T(4,128)S(1)}, s32[4,256]{1,0:T(4,128)}, u32[]{:S(2)}) copy-start(s32[4,256]{1,0:T(4,128)} %param.11) | copy-start | bytes 12292
  5.5 22.9 %copy-start.1 = (f32[1,80,4,256]{3,1,2,0:T(8,128)}, f32[1,80,4,256]{3,1,2,0:T(8,128)S(1)}, u32[]{:S(2)}) copy-start(f32[1,80,4,256]{3,1,2,0:T(8,128)S(1)} %get-tuple-element.1095) | copy-start | bytes 983044
  5.5 22.9 %copy-start.2 = (f32[1,80,4,256]{3,1,2,0:T(8,128)}, f32[1,80,4,256]{3,1,2,0:T(8,128)S(1)}, u32[]{:S(2)}) copy-start(f32[1,80,4,256]{3,1,2,0:T(8,128)S(1)} %get-tuple-element.1096) | copy-start | bytes 983044
  6.8 21.6 %collective-permute-start.4 = (f32[7,80,1,256]{3,1,2,0:T(8,128)}, f32[7,80,1,256]{3,1,2,0:T(8,128)S(1)}, u32[]{:S(2)}, u32[]{:S(2)}) collective-permute-start(f32[7,80,1,256]{3,1,2,0:T(8,128)} %get-tuple-element.1068), channel_id=1, source_target_pairs={{0,16},{16,32},{32,48},{48,64},{64,80},{80,96},{96,112},{112,128},... | collective-permute-start | bytes 1720328 | tf_op jit(solution)/shard_map/ppermute | solution.py:19
  6.8 21.6 %collective-permute-start.5 = (f32[7,80,1,256]{3,1,2,0:T(8,128)}, f32[7,80,1,256]{3,1,2,0:T(8,128)S(1)}, u32[]{:S(2)}, u32[]{:S(2)}) collective-permute-start(f32[7,80,1,256]{3,1,2,0:T(8,128)} %get-tuple-element.1069), channel_id=1, source_target_pairs={{16,0},{32,16},{48,32},{64,48},{80,64},{96,80},{112,96},{128,112},... | collective-permute-start | bytes 1720328 | tf_op jit(solution)/shard_map/ppermute | solution.py:21
  9.4 1.8 %copy-start.8 = (s32[1,80,1,256]{3,1,2,0:T(8,128)}, s32[1,80,1,256]{3,1,2,0:T(8,128)S(1)}, u32[]{:S(2)}) copy-start(s32[1,80,1,256]{3,1,2,0:T(8,128)S(1)} %collective-permute-done) | copy-start | bytes 245764
  9.5 1.7 %copy-start.10 = (s32[1,80,1,256]{3,1,2,0:T(8,128)}, s32[1,80,1,256]{3,1,2,0:T(8,128)S(1)}, u32[]{:S(2)}) copy-start(s32[1,80,1,256]{3,1,2,0:T(8,128)S(1)} %collective-permute-done.1) | copy-start | bytes 245764
  11.2 13.4 %collective-permute-start.2 = (s32[1,80,6,1]{3,1,2,0:T(8,128)}, s32[1,80,6,1]{3,1,2,0:T(8,128)}, u32[]{:S(2)}, u32[]{:S(2)}) collective-permute-start(s32[1,80,6,1]{3,1,2,0:T(8,128)} %get-tuple-element.1077), channel_id=1, source_target_pairs={{0,1},{1,2},{2,3},{3,4},{4,5},{5,6},{6,7},{7,8},{8,9},{9,10},{10,1... | collective-permute-start | bytes 5768 | tf_op jit(solution)/shard_map/ppermute | solution.py:19
  13.4 11.2 %collective-permute-start.3 = (s32[1,80,6,1]{3,1,2,0:T(8,128)}, s32[1,80,6,1]{3,1,2,0:T(8,128)}, u32[]{:S(2)}, u32[]{:S(2)}) collective-permute-start(s32[1,80,6,1]{3,1,2,0:T(8,128)} %get-tuple-element.1078), channel_id=1, source_target_pairs={{1,0},{2,1},{3,2},{4,3},{5,4},{6,5},{7,6},{8,7},{9,8},{10,9},{11,1... | collective-permute-start | bytes 5768 | tf_op jit(solution)/shard_map/ppermute | solution.py:21
  28.4 0.9 copy-start.5
  29.3 0.8 copy-start.6
  30.3 8.6 %copy-start.7 = (pred[80,6,258]{2,0,1:T(8,128)(4,1)S(1)}, pred[80,6,258]{2,0,1:T(8,128)(4,1)}, u32[]{:S(2)}) copy-start(pred[80,6,258]{2,0,1:T(8,128)(4,1)} %get-tuple-element.1036) | copy-start | bytes 371524
  35.8 10.7 %collective-permute-start.7 = (f32[7,80,6,1]{1,3,2,0:T(1,128)}, f32[7,80,6,1]{1,3,2,0:T(1,128)}, u32[]{:S(2)}, u32[]{:S(2)}) collective-permute-start(f32[7,80,6,1]{1,3,2,0:T(1,128)} %copy.23), channel_id=1, source_target_pairs={{1,0},{2,1},{3,2},{4,3},{5,4},{6,5},{7,6},{8,7},{9,8},{10,9},{11,1... | collective-permute-start | bytes 40328 | tf_op jit(solution)/shard_map/ppermute | solution.py:21
  38.0 7.2 %collective-permute-start.6 = (f32[7,80,6,1]{1,3,2,0:T(1,128)}, f32[7,80,6,1]{1,3,2,0:T(1,128)}, u32[]{:S(2)}, u32[]{:S(2)}) collective-permute-start(f32[7,80,6,1]{1,3,2,0:T(1,128)} %copy.22), channel_id=1, source_target_pairs={{0,1},{1,2},{2,3},{3,4},{4,5},{5,6},{6,7},{7,8},{8,9},{9,10},{10,1... | collective-permute-start | bytes 40328 | tf_op jit(solution)/shard_map/ppermute | solution.py:19
  49.0 5.6 %copy-start = (f32[5,80,6,258]{3,1,2,0:T(8,128)S(1)}, f32[5,80,6,258]{3,1,2,0:T(8,128)}, u32[]{:S(2)}) copy-start(f32[5,80,6,258]{3,1,2,0:T(8,128)} %select_select_fusion) | copy-start | bytes 7430404
  49.0 5.6 %copy-start.4 = (s32[1,80,4,256]{3,1,2,0:T(8,128)S(1)}, s32[1,80,4,256]{3,1,2,0:T(8,128)}, u32[]{:S(2)}) copy-start(s32[1,80,4,256]{3,1,2,0:T(8,128)} %copy-done.3) | copy-start | bytes 983044
  49.0 5.6 %copy-start.9 = (s32[1,80,1,256]{3,1,2,0:T(8,128)S(1)}, s32[1,80,1,256]{3,1,2,0:T(8,128)}, u32[]{:S(2)}) copy-start(s32[1,80,1,256]{3,1,2,0:T(8,128)} %copy-done.8) | copy-start | bytes 245764
  49.0 5.6 %copy-start.11 = (s32[1,80,1,256]{3,1,2,0:T(8,128)S(1)}, s32[1,80,1,256]{3,1,2,0:T(8,128)}, u32[]{:S(2)}) copy-start(s32[1,80,1,256]{3,1,2,0:T(8,128)} %copy-done.10) | copy-start | bytes 245764
  88.7 2.6 %copy-start.15 = (f32[5,4,256]{2,1,0:T(4,128)S(1)}, f32[5,4,256]{2,1,0:T(4,128)}, u32[]{:S(2)}) copy-start(f32[5,4,256]{2,1,0:T(4,128)} %param.9) | copy-start | bytes 61444
where the time goes:
time: 149 us
  blocking collectives  54.2 us (36%)
  other arithmetic  54.1 us (36%)
  local copies, waits for them, and re-layouts  15.4 us (10%)
  waiting for transfers between devices  10.6 us (7%)
  starting transfers between devices  8.82 us (6%)
  between operations  5.4 us (4%)
    psum x5, blocking collectives, over_axes(): value = lax.psum(value, axis)  54.2 us
    reduce_sum x2, other arithmetic, code_sums(): jnp.sum(jnp.where(hit, prod, 0.0), axis=0)  29.3 us
    ppermute x4, waiting for transfers between devices, extended_2(): lax.ppermute(tail, axis, [(i, (i + 1) % count) for i in range(count)])  10.6 us
    concatenate x3, other arithmetic, extended_2(): jnp.concatenate([lax.ppermute(tail, axis, [(i, (i + 1) % count) for i in...  6.65 us
    ppermute x4, starting transfers between devices, extended_2(): lax.ppermute(head, axis, [((i + 1) % count, i) for i in range(count)])  5.65 us
    select_n x1, other arithmetic, code_sums(): source = jnp.where((codes == code)[None], windows[code][:, None], source)  5.64 us
    slice x4, local copies, waits for them, and re-layouts, extended_2(): lax.slice_in_dim(cells, cells.shape[dim] - width, cells.shape[dim], axis=...  5.24 us
    unnamed x209, local copies, waits for them, and re-layouts  4.1 us
  transfers between devices with their start and end apart: 8, of which 2 were waited for; matrix products, arithmetic and copies ran while one was open for 11% of the time, Pallas kernels for 0%

commit v1 on v0

--- a/solution.py
+++ b/solution.py
@@ -27,7 +27,7 @@
 
 def over_axes(value, axes):
     for axis in axes:
-        value = lax.psum(value, axis)
+        value = jnp.sum(lax.all_gather(value, axis), axis=0)
     return value
 
 

time: 149 us -> 213 us (1.43)
  local copies, waits for them, and re-layouts: 15.4 us -> 79.4 us
  other arithmetic: 54.1 us -> 61.5 us
  waiting for transfers between devices: 10.6 us -> 6.74 us
  blocking collectives: 54.2 us -> 50.9 us
    unnamed x209 -> x244, local copies, waits for them, and re-layouts: 4.1 us -> 65.7 us
    psum x5 -> x0, blocking collectives: 54.2 us -> none  [over_axes(): value = lax.psum(value, axis)]
    unnamed x0 -> x5, blocking collectives: none -> 50.9 us
    reduce_sum x0 -> x10, other arithmetic: none -> 6.09 us  [over_axes(): value = jnp.sum(lax.all_gather(value, axis), axis=0)]
    ppermute x4, waiting for transfers between devices: 10.6 us -> 6.73 us  [extended_2(): lax.ppermute(tail, axis, [(i, (i + 1) % count) for i in range(count)])]
    another operation x9, local copies, waits for them, and re-layouts: 0.03 us -> 2.41 us  [code_sums(): jnp.stack([jnp.sum(jnp.where(hit, prod, 0.0), axis=0) for prod in product...]
  transfers between devices with their start and end apart: 8 -> 8, of which waited for: 2 -> 2; matrix products, arithmetic and copies ran while one was open for 11% -> 10% of each run, Pallas kernels for 0% -> 0%
where the time goes in v1:
time: 213 us; the launch traced here: 212 us
  local copies, waits for them, and re-layouts  79.4 us (37%)
  other arithmetic  61.5 us (29%)
  blocking collectives  50.9 us (24%)
  starting transfers between devices  8.82 us (4%)
  waiting for transfers between devices  6.74 us (3%)
  between operations  4.96 us (2%)
    unnamed x244, local copies, waits for them, and re-layouts  65.7 us
    unnamed x5, blocking collectives  50.9 us
    reduce_sum x2, other arithmetic, code_sums(): jnp.sum(jnp.where(hit, prod, 0.0), axis=0)  29.3 us
    ppermute x4, waiting for transfers between devices, extended_2(): lax.ppermute(tail, axis, [(i, (i + 1) % count) for i in range(count)])  6.73 us
    concatenate x3, other arithmetic, extended_2(): jnp.concatenate([lax.ppermute(tail, axis, [(i, (i + 1) % count) for i in...  6.65 us
    reduce_sum x10, other arithmetic, over_axes(): value = jnp.sum(lax.all_gather(value, axis), axis=0)  6.09 us
    ppermute x4, starting transfers between devices, extended_2(): lax.ppermute(head, axis, [((i + 1) % count, i) for i in range(count)])  5.65 us
    select_n x1, other arithmetic, code_sums(): source = jnp.where((codes == code)[None], windows[code][:, None], source)  5.64 us
  transfers between devices with their start and end apart: 8, of which 2 were waited for; matrix products, arithmetic and copies ran while one was open for 10% of the time, Pallas kernels for 0%

profile of v1, /device:TPU:14, one launch (start us, length us, event | category | flops | bytes accessed | tf_op | source)
XLA Modules:
  0.0 212.3 jit_solution(17299374893881362682)
XLA Ops:
  1.9 1.7 collective-permute-start.1
  3.6 1.7 copy.21
  6.8 1.7 collective-permute-start.5
  11.3 2.2 %collective-permute-start.2 = (s32[1,80,6,1]{3,1,2,0:T(8,128)}, s32[1,80,6,1]{3,1,2,0:T(8,128)}, u32[]{:S(2)}, u32[]{:S(2)}) collective-permute-start(s32[1,80,6,1]{3,1,2,0:T(8,128)} %get-tuple-element.1077), channel_id=1, source_target_pairs={{0,1},{1,2},{2,3},{3,4},{4,5},{5,6},{6,7},{7,8},{8,9},{9,10},{10,1... | collective-permute-start | bytes 5768 | tf_op jit(solution)/shard_map/ppermute | solution.py:19
  18.6 6.0 %collective-permute-done.2 = s32[1,80,6,1]{3,1,2,0:T(8,128)} collective-permute-done((s32[1,80,6,1]{3,1,2,0:T(8,128)}, s32[1,80,6,1]{3,1,2,0:T(8,128)}, u32[]{:S(2)}, u32[]{:S(2)}) %collective-permute-start.2) | collective-permute-done | bytes 1952 | tf_op jit(solution)/shard_map/ppermute | solution.py:19
  24.7 2.2 %broadcast_compare_fusion.11 = (pred[80,6,258]{2,0,1:T(8,128)(4,1)}, s32[80,6,258]{2,0,1:T(8,128)S(1)}) fusion(s32[80,6,1]{2,0,1:T(8,128)} %bitcast.13, s32[80,6,256]{2,0,1:T(8,128)} %get-tuple-element.1079, s32[80,6,1]{2,0,1:T(8,128)} %bitcast.11), kind=kLoop, calls=%fused_computation.445 | loop fusion | flops 371520 | bytes 1114560 | tf_op jit(solution)/shard_map/eq | solution.py:45
  26.9 1.6 broadcast_compare_fusion.10
  30.4 1.8 fusion.84
  32.1 2.6 %copy.22 = f32[7,80,6,1]{1,3,2,0:T(1,128)} copy(f32[7,80,6,1]{3,1,2,0:T(8,128)} %get-tuple-element.1066) | data formatting | bytes 26880 | tf_op jit(solution)/shard_map/slice | solution.py:16
  35.9 2.2 %collective-permute-start.7 = (f32[7,80,6,1]{1,3,2,0:T(1,128)}, f32[7,80,6,1]{1,3,2,0:T(1,128)}, u32[]{:S(2)}, u32[]{:S(2)}) collective-permute-start(f32[7,80,6,1]{1,3,2,0:T(1,128)} %copy.23), channel_id=1, source_target_pairs={{1,0},{2,1},{3,2},{4,3},{5,4},{6,5},{7,6},{8,7},{9,8},{10,9},{11,1... | collective-permute-start | bytes 40328 | tf_op jit(solution)/shard_map/ppermute | solution.py:21
  39.0 5.6 %select_select_fusion = f32[5,80,6,258]{3,1,2,0:T(8,128)} fusion(f32[5,6,258]{2,1,0:T(8,128)} %get-tuple-element.1094, f32[5,6,258]{2,1,0:T(8,128)} %get-tuple-element.1093, f32[5,6,258]{2,1,0:T(8,128)} %get-tuple-element.1092, f32[5,6,258]{2,1,0:T(8,128)} %get-tuple-element.1091, f32[5,6,258]{2,1,0:T(8,128)} %get-tuple-element.1090, ...), kind=kLoop, calls=%fused_computation.1 | loop fusion | flops 4953600 | bytes 3746160 | tf_op jit(solution)/shard_map/jit(_where)/select_n | solution.py:45
  45.3 1.3 copy.24
  46.6 2.5 %copy.25 = f32[7,80,6,1]{3,1,2,0:T(8,128)} copy(f32[7,80,6,1]{1,3,2,0:T(1,128)} %collective-permute-done.7) | data formatting | bytes 26880 | tf_op jit(solution)/shard_map/ppermute | solution.py:21
  49.1 5.6 %pad_maximum_fusion = f32[7,80,6,258]{3,1,2,0:T(8,128)S(1)} fusion(f32[7,80,6,1]{3,1,2,0:T(8,128)} %copy.25, f32[7,80,1,256]{3,1,2,0:T(8,128)} %copy-done.6, f32[1,80,4,256]{3,1,2,0:T(8,128)} %copy-done.1, f32[1,80,4,256]{3,1,2,0:T(8,128)} %copy-done.2, f32[5,80,4,256]{3,1,2,0:T(8,128)S(1)} %copy.21, f32[7,80,1,256]{3,1,2,0:T(8,128)} %copy-done.5, ...), kind=kLoop, calls=%fused_computation | loop fusion | flops 5201280 | bytes 6935040 | tf_op jit(solution)/shard_map/concatenate | solution.py:17
  54.7 3.3 %multiply_reduce_fusion = (f32[]{:T(128)}, f32[80,6,258]{2,0,1:T(8,128)S(1)}, f32[80,6,258]{2,0,1:T(8,128)S(1)}, s32[1,80,6,258]{3,1,2,0:T(8,128)S(1)}) fusion(f32[7,80,6,258]{3,1,2,0:T(8,128)S(1)} %pad_maximum_fusion, s32[258]{0:T(512)S(1)} %iota_add_fusion, s32[6]{0:T(128)S(1)} %iota_add_fusion.1, s32[1,80,6,1]{3,1,2,0:T(8,128)} %collective-permute-done.3, ...), kind=kLoop, calls=%fused_computation.37 | loop fusion | flops 5325119 | bytes 7926820 | tf_op jit(solution)/shard_map/reduce_sum | solution.py:61
  59.4 15.2 %select_reduce_fusion.169 = (f32[6,258]{1,0:T(8,128)S(1)}, f32[6,258]{1,0:T(8,128)S(1)}, f32[6,258]{1,0:T(8,128)S(1)}, f32[6,258]{1,0:T(8,128)S(1)}, f32[6,258]{...) fusion(f32[80,6,258]{2,0,1:T(8,128)S(1)} %get-tuple-element.105, ...), kind=kLoop, calls=%fused_computation.207 | loop fusion | flops 23266440 | bytes 7120800 | tf_op jit(solution)/shard_map/reduce_sum | solution.py:59
  74.6 14.1 %select_reduce_fusion.179 = (f32[6,258]{1,0:T(8,128)S(1)}, f32[6,258]{1,0:T(8,128)S(1)}, f32[6,258]{1,0:T(8,128)S(1)}, f32[6,258]{1,0:T(8,128)S(1)}, f32[6,258]{...) fusion(f32[80,6,258]{2,0,1:T(8,128)S(1)} %get-tuple-element.106, ...), kind=kLoop, calls=%fused_computation.217 | loop fusion | flops 22151880 | bytes 6625440 | tf_op jit(solution)/shard_map/reduce_sum | solution.py:59
  91.1 1.5 dynamic-update-slice
  92.7 6.4 %all-reduce.15 = (f32[2]{0:T(128)S(1)}, f32[2]{0:T(128)S(1)}) all-reduce(f32[2]{0:T(128)S(1)} %dynamic-update-slice, f32[2]{0:T(128)S(1)} %dynamic-update-slice.5), channel_id=1, replica_groups=mesh['ra_0'=2,'ra_1'=4,'ra_2'=2,'dec_0'=8,'dec_1'=2] {'ra_0'}, use_global_device_ids=true, to_apply=%add.1 | all-reduce | flops 4 | bytes 32
  100.4 1.4 dynamic-update-slice.6
  101.8 1.4 dynamic-update-slice.1
  103.3 16.7 %all-reduce.12 = (f32[4]{0:T(128)S(1)}, f32[4]{0:T(128)S(1)}) all-reduce(f32[4]{0:T(128)S(1)} %dynamic-update-slice.1, f32[4]{0:T(128)S(1)} %dynamic-update-slice.6), channel_id=1, replica_groups=mesh['ra_0'=2,'ra_1'=4,'ra_2'=2,'dec_0'=8,'dec_1'=2] {'ra_1'}, use_global_device_ids=true, to_apply=%add.2 | all-reduce | flops 8 | bytes 64
  121.2 1.4 dynamic-update-slice.7
  122.6 1.4 dynamic-update-slice.2
  123.9 2.4 %all-reduce.14 = (f32[2]{0:T(128)S(1)}, f32[2]{0:T(128)S(1)}) all-reduce(f32[2]{0:T(128)S(1)} %dynamic-update-slice.2, f32[2]{0:T(128)S(1)} %dynamic-update-slice.7), channel_id=1, replica_groups=mesh['ra_0'=2,'ra_1'=4,'ra_2'=2,'dec_0'=8,'dec_1'=2] {'ra_2'}, use_global_device_ids=true, to_apply=%add.3 | all-reduce | flops 4 | bytes 32
  127.6 1.3 dynamic-update-slice.8
  128.9 1.3 dynamic-update-slice.3
  176.8 1.6 slice_add_fusion
  178.4 20.4 %all-reduce.11 = (f32[8]{0:T(128)S(1)}, f32[8]{0:T(128)S(1)}) all-reduce(f32[8]{0:T(128)S(1)} %dynamic-update-slice.3, f32[8]{0:T(128)S(1)} %dynamic-update-slice.8), channel_id=1, replica_groups=mesh['ra_0'=2,'ra_1'=4,'ra_2'=2,'dec_0'=8,'dec_1'=2] {'dec_0'}, use_global_device_ids=true, to_apply=%add.4 | all-reduce | flops 16 | bytes 128
  200.0 1.4 dynamic-update-slice.9
  201.4 1.4 dynamic-update-slice.4
  203.6 4.9 %all-reduce.13 = (f32[2]{0:T(128)S(1)}, f32[2]{0:T(128)S(1)}) all-reduce(f32[2]{0:T(128)S(1)} %dynamic-update-slice.4, f32[2]{0:T(128)S(1)} %dynamic-update-slice.9), channel_id=1, replica_groups=mesh['ra_0'=2,'ra_1'=4,'ra_2'=2,'dec_0'=8,'dec_1'=2] {'dec_1'}, use_global_device_ids=true, to_apply=%add.5 | all-reduce | flops 4 | bytes 32
  (283 shorter events, 70.9 us)
Async XLA Ops:
  0.6 4.7 %copy-start.12 = (f32[80,4,256]{2,1,0:T(4,128)S(1)}, f32[80,4,256]{2,1,0:T(4,128)}, u32[]{:S(2)}) copy-start(f32[80,4,256]{2,1,0:T(4,128)} %param.8) | copy-start | bytes 983044
  0.6 4.7 %copy-start.13 = (f32[80,4,256]{2,1,0:T(4,128)S(1)}, f32[80,4,256]{2,1,0:T(4,128)}, u32[]{:S(2)}) copy-start(f32[80,4,256]{2,1,0:T(4,128)} %param.7) | copy-start | bytes 983044
  1.8 7.8 %copy-start.3 = (s32[1,80,4,256]{3,1,2,0:T(8,128)}, s32[1,80,4,256]{3,1,2,0:T(8,128)S(1)}, u32[]{:S(2)}) copy-start(s32[1,80,4,256]{3,1,2,0:T(8,128)S(1)} %fusion.38) | copy-start | bytes 983044
  1.8 7.7 %collective-permute-start = (s32[1,80,1,256]{3,1,2,0:T(8,128)S(1)}, s32[1,80,1,256]{3,1,2,0:T(8,128)S(1)}, u32[]{:S(2)}, u32[]{:S(2)}) collective-permute-start(s32[1,80,1,256]{3,1,2,0:T(8,128)S(1)} %get-tuple-element.1081), channel_id=1, source_target_pairs={{0,16},{16,32},{32,48},{48,64},{64,80},{80,96},{96,112},{112,128},... | collective-permute-start | bytes 245768 | tf_op jit(solution)/shard_map/ppermute | solution.py:19
  1.9 6.7 %copy-start.14 = (f32[5,4,256]{2,1,0:T(4,128)S(1)}, f32[5,4,256]{2,1,0:T(4,128)}, u32[]{:S(2)}) copy-start(f32[5,4,256]{2,1,0:T(4,128)} %param.9) | copy-start | bytes 61444
  1.9 7.6 %collective-permute-start.1 = (s32[1,80,1,256]{3,1,2,0:T(8,128)S(1)}, s32[1,80,1,256]{3,1,2,0:T(8,128)S(1)}, u32[]{:S(2)}, u32[]{:S(2)}) collective-permute-start(s32[1,80,1,256]{3,1,2,0:T(8,128)S(1)} %get-tuple-element.1082), channel_id=1, source_target_pairs={{16,0},{32,16},{48,32},{64,48},{80,64},{96,80},{112,96},{128,112},... | collective-permute-start | bytes 245768 | tf_op jit(solution)/shard_map/ppermute | solution.py:21
  5.4 8.1 %copy-start.16 = (s32[4,256]{1,0:T(4,128)S(1)}, s32[4,256]{1,0:T(4,128)}, u32[]{:S(2)}) copy-start(s32[4,256]{1,0:T(4,128)} %param.11) | copy-start | bytes 12292
  5.4 9.4 %copy-start.21 = (u32[256]{0:T(256)S(1)}, u32[256]{0:T(256)}, u32[]{:S(2)}) copy-start(u32[256]{0:T(256)} %constant.81) | copy-start | bytes 3076
  5.4 10.0 %copy-start.20 = (u32[256]{0:T(256)S(1)}, u32[256]{0:T(256)}, u32[]{:S(2)}) copy-start(u32[256]{0:T(256)} %constant.76) | copy-start | bytes 3076
  5.4 10.5 %copy-start.19 = (u32[256]{0:T(256)S(1)}, u32[256]{0:T(256)}, u32[]{:S(2)}) copy-start(u32[256]{0:T(256)} %constant.71) | copy-start | bytes 3076
  5.4 11.2 %copy-start.18 = (u32[256]{0:T(256)S(1)}, u32[256]{0:T(256)}, u32[]{:S(2)}) copy-start(u32[256]{0:T(256)} %constant.66) | copy-start | bytes 3076
  5.4 11.8 %copy-start.17 = (u32[256]{0:T(256)S(1)}, u32[256]{0:T(256)}, u32[]{:S(2)}) copy-start(u32[256]{0:T(256)} %constant.61) | copy-start | bytes 3076
  5.6 22.9 %copy-start.1 = (f32[1,80,4,256]{3,1,2,0:T(8,128)}, f32[1,80,4,256]{3,1,2,0:T(8,128)S(1)}, u32[]{:S(2)}) copy-start(f32[1,80,4,256]{3,1,2,0:T(8,128)S(1)} %get-tuple-element.1095) | copy-start | bytes 983044
  5.6 22.9 %copy-start.2 = (f32[1,80,4,256]{3,1,2,0:T(8,128)}, f32[1,80,4,256]{3,1,2,0:T(8,128)S(1)}, u32[]{:S(2)}) copy-start(f32[1,80,4,256]{3,1,2,0:T(8,128)S(1)} %get-tuple-element.1096) | copy-start | bytes 983044
  6.8 21.6 %collective-permute-start.4 = (f32[7,80,1,256]{3,1,2,0:T(8,128)}, f32[7,80,1,256]{3,1,2,0:T(8,128)S(1)}, u32[]{:S(2)}, u32[]{:S(2)}) collective-permute-start(f32[7,80,1,256]{3,1,2,0:T(8,128)} %get-tuple-element.1068), channel_id=1, source_target_pairs={{0,16},{16,32},{32,48},{48,64},{64,80},{80,96},{96,112},{112,128},... | collective-permute-start | bytes 1720328 | tf_op jit(solution)/shard_map/ppermute | solution.py:19
  6.8 21.6 %collective-permute-start.5 = (f32[7,80,1,256]{3,1,2,0:T(8,128)}, f32[7,80,1,256]{3,1,2,0:T(8,128)S(1)}, u32[]{:S(2)}, u32[]{:S(2)}) collective-permute-start(f32[7,80,1,256]{3,1,2,0:T(8,128)} %get-tuple-element.1069), channel_id=1, source_target_pairs={{16,0},{32,16},{48,32},{64,48},{80,64},{96,80},{112,96},{128,112},... | collective-permute-start | bytes 1720328 | tf_op jit(solution)/shard_map/ppermute | solution.py:21
  9.5 1.8 copy-start.8
  9.5 1.7 copy-start.10
  11.3 13.4 %collective-permute-start.2 = (s32[1,80,6,1]{3,1,2,0:T(8,128)}, s32[1,80,6,1]{3,1,2,0:T(8,128)}, u32[]{:S(2)}, u32[]{:S(2)}) collective-permute-start(s32[1,80,6,1]{3,1,2,0:T(8,128)} %get-tuple-element.1077), channel_id=1, source_target_pairs={{0,1},{1,2},{2,3},{3,4},{4,5},{5,6},{6,7},{7,8},{8,9},{9,10},{10,1... | collective-permute-start | bytes 5768 | tf_op jit(solution)/shard_map/ppermute | solution.py:19
  13.4 11.2 %collective-permute-start.3 = (s32[1,80,6,1]{3,1,2,0:T(8,128)}, s32[1,80,6,1]{3,1,2,0:T(8,128)}, u32[]{:S(2)}, u32[]{:S(2)}) collective-permute-start(s32[1,80,6,1]{3,1,2,0:T(8,128)} %get-tuple-element.1078), channel_id=1, source_target_pairs={{1,0},{2,1},{3,2},{4,3},{5,4},{6,5},{7,6},{8,7},{9,8},{10,9},{11,1... | collective-permute-start | bytes 5768 | tf_op jit(solution)/shard_map/ppermute | solution.py:21
  28.5 0.9 copy-start.5
  29.3 0.8 copy-start.6
  30.4 8.6 %copy-start.7 = (pred[80,6,258]{2,0,1:T(8,128)(4,1)S(1)}, pred[80,6,258]{2,0,1:T(8,128)(4,1)}, u32[]{:S(2)}) copy-start(pred[80,6,258]{2,0,1:T(8,128)(4,1)} %get-tuple-element.1036) | copy-start | bytes 371524
  35.9 10.7 %collective-permute-start.7 = (f32[7,80,6,1]{1,3,2,0:T(1,128)}, f32[7,80,6,1]{1,3,2,0:T(1,128)}, u32[]{:S(2)}, u32[]{:S(2)}) collective-permute-start(f32[7,80,6,1]{1,3,2,0:T(1,128)} %copy.23), channel_id=1, source_target_pairs={{1,0},{2,1},{3,2},{4,3},{5,4},{6,5},{7,6},{8,7},{9,8},{10,9},{11,1... | collective-permute-start | bytes 40328 | tf_op jit(solution)/shard_map/ppermute | solution.py:21
  38.1 7.2 %collective-permute-start.6 = (f32[7,80,6,1]{1,3,2,0:T(1,128)}, f32[7,80,6,1]{1,3,2,0:T(1,128)}, u32[]{:S(2)}, u32[]{:S(2)}) collective-permute-start(f32[7,80,6,1]{1,3,2,0:T(1,128)} %copy.22), channel_id=1, source_target_pairs={{0,1},{1,2},{2,3},{3,4},{4,5},{5,6},{6,7},{7,8},{8,9},{9,10},{10,1... | collective-permute-start | bytes 40328 | tf_op jit(solution)/shard_map/ppermute | solution.py:19
  49.1 5.6 %copy-start = (f32[5,80,6,258]{3,1,2,0:T(8,128)S(1)}, f32[5,80,6,258]{3,1,2,0:T(8,128)}, u32[]{:S(2)}) copy-start(f32[5,80,6,258]{3,1,2,0:T(8,128)} %select_select_fusion) | copy-start | bytes 7430404
  49.1 5.6 %copy-start.4 = (s32[1,80,4,256]{3,1,2,0:T(8,128)S(1)}, s32[1,80,4,256]{3,1,2,0:T(8,128)}, u32[]{:S(2)}) copy-start(s32[1,80,4,256]{3,1,2,0:T(8,128)} %copy-done.3) | copy-start | bytes 983044
  49.1 5.6 %copy-start.9 = (s32[1,80,1,256]{3,1,2,0:T(8,128)S(1)}, s32[1,80,1,256]{3,1,2,0:T(8,128)}, u32[]{:S(2)}) copy-start(s32[1,80,1,256]{3,1,2,0:T(8,128)} %copy-done.8) | copy-start | bytes 245764
  49.1 5.6 %copy-start.11 = (s32[1,80,1,256]{3,1,2,0:T(8,128)S(1)}, s32[1,80,1,256]{3,1,2,0:T(8,128)}, u32[]{:S(2)}) copy-start(s32[1,80,1,256]{3,1,2,0:T(8,128)} %copy-done.10) | copy-start | bytes 245764
  88.7 114.2 %copy-start.15 = (f32[5,4,256]{2,1,0:T(4,128)S(1)}, f32[5,4,256]{2,1,0:T(4,128)}, u32[]{:S(2)}) copy-start(f32[5,4,256]{2,1,0:T(4,128)} %param.9) | copy-start | bytes 61444
